TPU v7x, 512 devices: a whole 4x4x16 slice. The times are simulated.
512 devices in a mesh: level: 16 (over z), dev: 32 (over x, y, core).
Axes of the slice: x: 4, y: 4, z: 16, core: 2. Of those that a mesh axis runs over, the one named last changes fastest.
Arguments:
- fields: float32 [16, 512, 12, 128], P('level', 'dev'), may hold values from -6 to 6
- own_src: int32 [16, 512], P('level', 'dev'), may hold values from 0 to 15
- own_weight: bfloat16 [16, 512, 128, 128], P('level', 'dev'), may hold values from 0 to 1, as said below
- send_block: int32 [16, 32, 32, 2], P('level', 'dev'), may hold values from 0 to 15
- send_target: int32 [16, 32, 32, 2], P('level', 'dev'), may hold values from 0 to 15
- send_count: int32 [16, 32, 32], P('level', 'dev'), may hold values from 0 to 2, as said below
- send_weight: bfloat16 [16, 32, 32, 2, 128, 128], P('level', 'dev'), may hold values from 0 to 1, as said below
- left_block: int32 [16, 32, 16, 2], P('level', 'dev'), may hold values from 0 to 15
- left_target: int32 [16, 32, 16, 2], P('level', 'dev'), may hold values from 0 to 15
- left_count: int32 [16, 32, 16], P('level', 'dev'), may hold values from 0 to 2, as said below
- left_weight: bfloat16 [16, 32, 16, 2, 128, 128], P('level', 'dev'), may hold values from 0 to 1, as said below
Outputs:
- remapped: float32 [16, 512, 12, 128], P('level', 'dev')
- totals: float32 [12], replicated
Inputs may be any that keep to these rules, and one draw needn't show every extreme that they name: send_count[l, s, s] = 0; for every level some receiver device gets 2 live slots from every other device of the level. left_count[m, q, m] = 0; for every device index some receiver level gets 2 live slots from every other level. `own_weight`: nonnegative; entry [k, i] is zero where old cell k and new cell i differ by more than 3; each column sums to a positive intersect fraction of at most 1. `send_weight`: nonnegative; entry [k, i] is zero where old cell k and new cell i differ by more than 3; each column sums to a positive intersect fraction of at most 1. `left_weight`: nonnegative; entry [k, i] is zero where old cell k and new cell i differ by more than 3; each column sums to a positive intersect fraction of at most 1.
All inputs are finite; a program needn't handle non-finite values.
Results may differ from a plain program's by a relative error of at most 0.0045.
Values may be sent and summed in bfloat16 or wider, within the bound.
No kernel may reach another device: no remote copies, remote signals or barrier semaphores. Data moves between devices by JAX's collectives and lax.ppermute only.
A program may use at most 64 MiB of HBM per device.

v0:
```python
import jax
import jax.numpy as jnp
from jax import lax
from jax.sharding import Mesh
from jax.sharding import PartitionSpec as P

DEV = ("dev_0", "dev_1", "dev_2")
LEVEL_DEV = ("level", "dev_0", "dev_1", "dev_2")


def one_axis_at_a_time(shard, axes):
    for axis in axes:
        shard = lax.psum(shard, axis)
    return shard


def pick_donors(rounded, block_index, count):
    donors = rounded[block_index]
    slots = block_index.shape[1]
    valid = lax.broadcasted_iota(jnp.int32, (1, slots), 1) < count[:, None]
    return jnp.where(valid[:, :, None, None], donors, jnp.zeros_like(donors))


def apply_weights(donors, weights):
    return jnp.einsum("pcmk,pcki->pcmi", donors, weights, preferred_element_type=jnp.float32)


def place_terms(contrib, target, blocks):
    comp = contrib.shape[2]
    cells = contrib.shape[3]
    flat_target = target.reshape(-1)
    onehot = (flat_target[:, None] == lax.broadcasted_iota(jnp.int32, (1, blocks), 1)).astype(
        jnp.float32
    )
    return jnp.einsum("sb,smi->bmi", onehot, contrib.reshape(-1, comp, cells))


def body(
    fields,
    own_src,
    own_weight,
    send_block,
    send_target,
    send_count,
    send_weight,
    left_block,
    left_target,
    left_count,
    left_weight,
):
    local = fields[0]
    blocks = local.shape[0]
    rounded = local.astype(jnp.bfloat16)
    own = jnp.einsum(
        "bmk,bki->bmi", rounded[own_src[0]], own_weight[0], preferred_element_type=jnp.float32
    )
    donors = pick_donors(rounded, send_block[0, 0], send_count[0, 0])
    strays = pick_donors(rounded, left_block[0, 0], left_count[0, 0])
    intra_terms, intra_target = (
        lax.all_to_all(
            apply_weights(donors, send_weight[0, 0]), DEV, split_axis=0, concat_axis=0, tiled=True
        ),
        lax.all_to_all(send_target[0, 0], DEV, split_axis=0, concat_axis=0, tiled=True),
    )
    left_terms, left_where = (
        lax.all_to_all(
            apply_weights(strays, left_weight[0, 0]),
            "level",
            split_axis=0,
            concat_axis=0,
            tiled=True,
        ),
        lax.all_to_all(left_target[0, 0], "level", split_axis=0, concat_axis=0, tiled=True),
    )
    remapped = (
        own
        + place_terms(intra_terms, intra_target, blocks)
        + place_terms(left_terms, left_where, blocks)
    )
    sums = one_axis_at_a_time(jnp.sum(remapped, axis=(0, 2)), LEVEL_DEV)
    totals = sums / (remapped.shape[2] * blocks)
    return (remapped[None], totals)


def solution(mesh):
    split = Mesh(
        mesh.devices.reshape(mesh.shape["level"], 4, 4, 2), ("level", "dev_0", "dev_1", "dev_2")
    )
    return jax.shard_map(
        body,
        mesh=split,
        in_specs=(
            P("level", DEV, None, None),
            P("level", DEV),
            P("level", DEV, None, None),
            P("level", DEV, None, None),
            P("level", DEV, None, None),
            P("level", DEV, None),
            P("level", DEV, None, None, None, None),
            P("level", DEV, None, None),
            P("level", DEV, None, None),
            P("level", DEV, None),
            P("level", DEV, None, None, None, None),
        ),
        out_specs=(P("level", DEV, None, None), P()),
        check_vma=False,
    )
```

profile of v0, /device:TPU:1, one launch (start us, length us, event | category | flops | bytes accessed | tf_op | source)
XLA Modules:
  0.0 132.4 jit_solution(2667217288526061684)
XLA Ops:
  0.7 1.5 %copy.36 = s32[32,1,2]{2,1,0:T(1,128)} copy(s32[32,1,2]{0,2,1:T(2,128)} %bitcast.52) | data formatting | bytes 512 | tf_op jit(solution)/shard_map/all_to_all | solution.py:63
  2.2 10.3 %all-to-all-start = ((s32[32,1,2]{2,1,0:T(1,128)}), s32[32,1,2]{2,1,0:T(1,128)S(1)}, u32[]{:S(2)}, u32[]{:S(2)}) async-start(s32[32,1,2]{2,1,0:T(1,128)} %copy.36), calls=%async_computation | async-start | bytes 32768 | tf_op jit(solution)/shard_map/all_to_all | solution.py:63
  12.5 0.9 copy.52
  14.3 0.7 iota_compare_fusion
  15.7 1.3 iota_compare_fusion.1
  17.0 1.3 gather_fusion.1
  18.4 1.6 %fusion = bf16[32,2,12,128]{3,2,1,0:T(8,128)(2,1)S(1)} fusion(bf16[1,1,32,2,128,128]{5,4,3,2,1,0:T(8,128)(2,1)S(1)} %copy-done, bf16[32,2,12,128]{3,2,1,0:T(8,128)(2,1)} %bitcast.47, pred[32,2]{1,0:T(8,128)(4,1)S(1)} %iota_compare_fusion), kind=kOutput, calls=%fused_computation.3 | convolution fusion | flops 25264128 | bytes 2490432 | tf_op jit(solution)/shard_map/pcmk,pcki->pcmi/dot_general | solution.py:25
  20.9 13.2 %all-to-all-start.2 = ((s32[16,1,2]{2,1,0:T(1,128)}), s32[16,1,2]{2,1,0:T(1,128)}, u32[]{:S(2)}, u32[]{:S(2)}) async-start(s32[16,1,2]{2,1,0:T(1,128)} %copy.41), calls=%async_computation.2 | async-start | bytes 16384 | tf_op jit(solution)/shard_map/all_to_all | solution.py:73
  34.7 0.8 copy.38
  35.5 0.7 gather_fusion.2
  36.2 9.0 %all-to-all-done.2 = s32[16,1,2]{2,1,0:T(1,128)} async-done(((s32[16,1,2]{2,1,0:T(1,128)}), s32[16,1,2]{2,1,0:T(1,128)}, u32[]{:S(2)}, u32[]{:S(2)}) %all-to-all-start.2) | async-done | bytes 160 | tf_op jit(solution)/shard_map/all_to_all | solution.py:73
  45.3 9.0 %all-to-all-start.1 = ((bf16[32,2,12,128]{3,1,2,0:T(2,128)(2,1)}), bf16[32,2,12,128]{3,1,2,0:T(2,128)(2,1)S(1)}, u32[]{:S(2)}, u32[]{:S(2)}) async-start(bf16[32,2,12,128]{3,1,2,0:T(2,128)(2,1)} %copy.38), calls=%async_computation.1 | async-start | bytes 393216 | tf_op jit(solution)/shard_map/all_to_all | solution.py:60
  54.3 1.1 fusion.3
  55.4 0.7 copy.43
  56.2 6.5 %all-to-all-done.1 = bf16[32,2,12,128]{3,1,2,0:T(2,128)(2,1)S(1)} async-done(((bf16[32,2,12,128]{3,1,2,0:T(2,128)(2,1)}), bf16[32,2,12,128]{3,1,2,0:T(2,128)(2,1)S(1)}, u32[]{:S(2)}, u32[]{:S(2)}) %all-to-all-start.1) | async-done | bytes 196640 | tf_op jit(solution)/shard_map/all_to_all | solution.py:60
  62.6 3.5 %all-to-all-start.3 = ((bf16[16,2,12,128]{3,1,2,0:T(2,128)(2,1)}), bf16[16,2,12,128]{3,1,2,0:T(2,128)(2,1)S(1)}, u32[]{:S(2)}, u32[]{:S(2)}) async-start(bf16[16,2,12,128]{3,1,2,0:T(2,128)(2,1)} %copy.43), calls=%async_computation.3 | async-start | bytes 196608 | tf_op jit(solution)/shard_map/all_to_all | solution.py:66
  67.9 0.7 reduce.7
  68.7 1.4 %reduce.6 = s32[16,2]{1,0:T(8,128)S(1)} reduce(s32[16,1,2]{2,1,0:T(1,128)} %all-to-all-done.2, s32[]{:T(128)} %broadcast.102), dimensions={1}, to_apply=%all_to_all.22.reduce_sub_computation.3 | reduce | bytes 260 | tf_op jit(solution)/shard_map/all_to_all | solution.py:73
  70.5 7.5 %all-to-all-done.3 = bf16[16,2,12,128]{3,1,2,0:T(2,128)(2,1)S(1)} async-done(((bf16[16,2,12,128]{3,1,2,0:T(2,128)(2,1)}), bf16[16,2,12,128]{3,1,2,0:T(2,128)(2,1)S(1)}, u32[]{:S(2)}, u32[]{:S(2)}) %all-to-all-start.3) | async-done | bytes 98336 | tf_op jit(solution)/shard_map/all_to_all | solution.py:66
  78.2 1.4 %fusion.24 = (f32[12]{0:T(128)S(1)}, f32[16,12,128]{2,1,0:T(8,128)S(1)}) fusion(f32[16,12,128]{2,0,1:T(8,128)S(1)} %fusion.17, f32[16,12,128]{2,0,1:T(8,128)S(1)} %fusion.14, bf16[16,12,128]{2,1,0:T(8,128)(2,1)S(1)} %gather_fusion, bf16[1,16,128,128]{3,2,1,0:T(8,128)(2,1)} %param.13), kind=kOutput, calls=%fused_computation.38 | convolution fusion | flops 6365172 | bytes 868400 | tf_op jit(solution)/shard_map/bmk,bki->bmi/dot_general | solution.py:54
  79.6 22.3 %psum.28 = f32[12]{0:T(128)S(1)} all-reduce(f32[12]{0:T(128)S(1)} %get-tuple-element.8), channel_id=1, replica_groups=mesh['level'=16,'dev_0'=4,'dev_1'=4,'dev_2'=2] {'level'}, use_global_device_ids=true, to_apply=%region_1.2 | all-reduce | flops 12 | bytes 96 | tf_op jit(solution)/shard_map/psum | solution.py:13
  101.9 6.8 %psum.29 = f32[12]{0:T(128)S(1)} all-reduce(f32[12]{0:T(128)S(1)} %psum.28), channel_id=1, replica_groups=mesh['level'=16,'dev_0'=4,'dev_1'=4,'dev_2'=2] {'dev_0'}, use_global_device_ids=true, to_apply=%region_2.3 | all-reduce | flops 12 | bytes 96 | tf_op jit(solution)/shard_map/psum | solution.py:13
  108.6 7.0 %psum.30 = f32[12]{0:T(128)S(1)} all-reduce(f32[12]{0:T(128)S(1)} %psum.29), channel_id=1, replica_groups=mesh['level'=16,'dev_0'=4,'dev_1'=4,'dev_2'=2] {'dev_1'}, use_global_device_ids=true, to_apply=%region_3.4 | all-reduce | flops 12 | bytes 96 | tf_op jit(solution)/shard_map/psum | solution.py:13
  116.3 15.6 %psum.31 = f32[12]{0:T(128)S(1)} all-reduce(f32[12]{0:T(128)S(1)} %psum.30), channel_id=1, replica_groups=mesh['level'=16,'dev_0'=4,'dev_1'=4,'dev_2'=2] {'dev_2'}, use_global_device_ids=true, to_apply=%region_4.5 | all-reduce | flops 12 | bytes 96 | tf_op jit(solution)/shard_map/psum | solution.py:13
  (28 shorter events, 6.7 us)
Async XLA Ops:
  0.6 17.7 %copy-start = (bf16[1,1,32,2,128,128]{5,4,3,2,1,0:T(8,128)(2,1)S(1)}, bf16[1,1,32,2,128,128]{5,4,3,2,1,0:T(8,128)(2,1)}, u32[]{:S(2)}) copy-start(bf16[1,1,32,2,128,128]{5,4,3,2,1,0:T(8,128)(2,1)} %param.17) | copy-start | bytes 6291460
  0.6 19.6 %copy-start.2 = (s32[1,1,16,2]{2,3,1,0:T(2,128)S(1)}, s32[1,1,16,2]{2,3,1,0:T(2,128)}, u32[]{:S(2)}) copy-start(s32[1,1,16,2]{2,3,1,0:T(2,128)} %param.19) | copy-start | bytes 388
  2.2 18.7 %all-to-all-start = ((s32[32,1,2]{2,1,0:T(1,128)}), s32[32,1,2]{2,1,0:T(1,128)S(1)}, u32[]{:S(2)}, u32[]{:S(2)}) async-start(s32[32,1,2]{2,1,0:T(1,128)} %copy.36), calls=%async_computation | async-start | bytes 32768 | tf_op jit(solution)/shard_map/all_to_all | solution.py:63
  17.0 37.3 %copy-start.1 = (bf16[1,1,16,2,128,128]{5,4,3,2,1,0:T(8,128)(2,1)S(1)}, bf16[1,1,16,2,128,128]{5,4,3,2,1,0:T(8,128)(2,1)}, u32[]{:S(2)}) copy-start(bf16[1,1,16,2,128,128]{5,4,3,2,1,0:T(8,128)(2,1)} %param.21) | copy-start | bytes 3145732
  20.9 24.4 %all-to-all-start.2 = ((s32[16,1,2]{2,1,0:T(1,128)}), s32[16,1,2]{2,1,0:T(1,128)}, u32[]{:S(2)}, u32[]{:S(2)}) async-start(s32[16,1,2]{2,1,0:T(1,128)} %copy.41), calls=%async_computation.2 | async-start | bytes 16384 | tf_op jit(solution)/shard_map/all_to_all | solution.py:73
  45.3 17.4 %all-to-all-start.1 = ((bf16[32,2,12,128]{3,1,2,0:T(2,128)(2,1)}), bf16[32,2,12,128]{3,1,2,0:T(2,128)(2,1)S(1)}, u32[]{:S(2)}, u32[]{:S(2)}) async-start(bf16[32,2,12,128]{3,1,2,0:T(2,128)(2,1)} %copy.38), calls=%async_computation.1 | async-start | bytes 393216 | tf_op jit(solution)/shard_map/all_to_all | solution.py:60
  62.6 15.4 %all-to-all-start.3 = ((bf16[16,2,12,128]{3,1,2,0:T(2,128)(2,1)}), bf16[16,2,12,128]{3,1,2,0:T(2,128)(2,1)S(1)}, u32[]{:S(2)}, u32[]{:S(2)}) async-start(bf16[16,2,12,128]{3,1,2,0:T(2,128)(2,1)} %copy.43), calls=%async_computation.3 | async-start | bytes 196608 | tf_op jit(solution)/shard_map/all_to_all | solution.py:66
where the time goes:
time: 133 us; the launch traced here: 132 us
  blocking collectives  51.6 us (39%)
  starting transfers between devices  36.1 us (27%)
  waiting for transfers between devices  23 us (17%)
  local copies, waits for them, and re-layouts  9.26 us (7%)
  other arithmetic  7.24 us (5%)
  matrix products  4.41 us (3%)
    psum x4, blocking collectives, one_axis_at_a_time(): shard = lax.psum(shard, axis)  51.6 us
    all_to_all x1, starting transfers between devices, body(): lax.all_to_all(left_target[0, 0], 'level', split_axis=0, concat_axis=0, t...  13.2 us
    all_to_all x1, starting transfers between devices, body(): lax.all_to_all(send_target[0, 0], DEV, split_axis=0, concat_axis=0, tiled...  10.3 us
    all_to_all x1, starting transfers between devices, body(): lax.all_to_all(apply_weights(donors, send_weight[0, 0]), DEV, split_axis=...  9.04 us
    all_to_all x1, waiting for transfers between devices, body(): lax.all_to_all(left_target[0, 0], 'level', split_axis=0, concat_axis=0, t...  9.02 us
    all_to_all x1, waiting for transfers between devices, body(): lax.all_to_all(apply_weights(strays, left_weight[0, 0]), 'level', split_a...  7.5 us
    all_to_all x1, waiting for transfers between devices, body(): lax.all_to_all(apply_weights(donors, send_weight[0, 0]), DEV, split_axis=...  6.46 us
    all_to_all x1, starting transfers between devices, body(): lax.all_to_all(apply_weights(strays, left_weight[0, 0]), 'level', split_a...  3.51 us
  transfers between devices with their start and end apart: 4, of which 3 were waited for; matrix products, arithmetic and copies ran while one was open for 13% of the time, Pallas kernels for 0%

commit v1 on v0

v1 whole, which is shorter than its diff:
```python
import functools

import jax
import jax.numpy as jnp
from jax import lax
from jax.experimental import pallas as pl
from jax.experimental.pallas import tpu as pltpu
from jax.sharding import Mesh
from jax.sharding import PartitionSpec as P

DEV = ("dev_0", "dev_1", "dev_2")
COMP = 12
CELLS = 128
BLK = 16
CAP = 2
ROWS = 32
GROUP = CELLS // ROWS
W_CHUNKS = 4
F32 = jnp.float32
BF16 = jnp.bfloat16


def code_tile(t0, t1, slot):
    row = lax.broadcasted_iota(jnp.int32, (8, CELLS), 0)
    lane = lax.broadcasted_iota(jnp.int32, (8, CELLS), 1)
    r = lane % ROWS
    here = (row == 0) & (lane // ROWS == slot)
    second = r >= COMP
    comp = jnp.where(second, r - COMP, r)
    code = comp * BLK + jnp.where(second, t1, t0)
    code = jnp.where(r < CAP * COMP, code, 255)
    return jnp.where(here, code, 0).astype(F32)


def three_parts(total):
    row = lax.broadcasted_iota(jnp.int32, (16, CELLS), 0)
    full = jnp.broadcast_to(total, (16, CELLS))
    hi = full.astype(BF16).astype(F32)
    mid = (full - hi).astype(BF16).astype(F32)
    low = full - hi - mid
    zero = jnp.zeros_like(full)
    return jnp.where(row == 9, hi, jnp.where(row == 10, mid, jnp.where(row == 11, low, zero)))


def sum_parts(tail):
    return tail[9:10] + tail[10:11] + tail[11:12]


def terms_kernel(
    place,
    fields,
    own_src,
    own_w,
    send_blk,
    send_tgt,
    send_cnt,
    send_w,
    left_blk,
    left_tgt,
    left_cnt,
    left_w,
    out_dev,
    out_lev,
    tail_lev,
    own_out,
    fld,
    first32,
    second32,
    first,
    second,
    wd,
    wl,
    wo,
    tail_dev,
    s_src,
    s_sblk,
    s_stgt,
    s_scnt,
    s_lblk,
    s_ltgt,
    s_lcnt,
    sems,
    wsems,
):
    peers = send_w.shape[0]
    levels = left_w.shape[0]
    small = []
    pairs = (
        (fields, fld),
        (own_src, s_src),
        (send_blk, s_sblk),
        (send_tgt, s_stgt),
        (send_cnt, s_scnt),
        (left_blk, s_lblk),
        (left_tgt, s_ltgt),
        (left_cnt, s_lcnt),
    )
    for n, (src, dst) in enumerate(pairs):
        copy = pltpu.make_async_copy(src, dst, sems.at[n])
        copy.start()
        small.append(copy)
    step = peers // W_CHUNKS
    weights = []
    for n in range(W_CHUNKS):
        sl = pl.ds(n * step, step)
        copy = pltpu.make_async_copy(send_w.at[sl], wd.at[sl], wsems.at[n])
        copy.start()
        weights.append(copy)
    left_copy = pltpu.make_async_copy(left_w, wl, wsems.at[W_CHUNKS])
    left_copy.start()
    own_copy = pltpu.make_async_copy(own_w, wo, wsems.at[W_CHUNKS + 1])
    own_copy.start()

    first32[...] = jnp.zeros(first32.shape, F32)
    second32[...] = jnp.zeros(second32.shape, F32)
    small[0].wait()
    for b in range(BLK):
        one = fld[pl.ds(b, COMP, stride=BLK), :]
        first32[b, 0:COMP, :] = one
        second32[b, COMP : 2 * COMP, :] = one
    first[...] = first32[...].astype(BF16)
    second[...] = second32[...].astype(BF16)
    for copy in small[1:]:
        copy.wait()

    def pair(blk, cnt, weight, n):
        live = cnt[0, n]
        b0 = jnp.where(live > 0, blk[0, n], BLK)
        b1 = jnp.where(live > 1, blk[1, n], BLK)
        lhs = jnp.concatenate([first[b0], second[b1]], axis=1)
        return jnp.dot(lhs, weight[n], preferred_element_type=F32)

    dev_slot = place[0] % GROUP
    lev_slot = place[1] % GROUP

    def dev_step(n, acc):
        t = pair(s_sblk, s_scnt, wd, n)
        out_dev[n, 0:16, :] = t[0:16].astype(BF16)
        tail_dev[n, 0:8, :] = t[16:24]
        tail_dev[n, 8:16, :] = code_tile(s_stgt[0, n], s_stgt[1, n], dev_slot)
        return acc + t[0:24]

    def lev_step(n, acc):
        t = pair(s_lblk, s_lcnt, wl, n)
        out_lev[n, 0:16, :] = t[0:16].astype(BF16)
        tail_lev[n, 0:8, :] = t[16:24]
        tail_lev[n, 8:16, :] = code_tile(s_ltgt[0, n], s_ltgt[1, n], lev_slot)
        return acc + t[0:24]

    acc = jnp.zeros((24, CELLS), F32)
    for n in range(W_CHUNKS):
        weights[n].wait()
        acc = lax.fori_loop(n * step, (n + 1) * step, dev_step, acc, unroll=True)
    left_copy.wait()
    acc = lax.fori_loop(0, levels, lev_step, acc, unroll=8)
    own_copy.wait()
    own_acc = jnp.zeros((16, CELLS), F32)
    for b in range(BLK):
        t = jnp.dot(first[s_src[0, b], 0:16, :], wo[b], preferred_element_type=F32)
        own_out[pl.ds(b, COMP, stride=BLK), :] = t[0:COMP]
        own_acc = own_acc + t
    own_acc = jnp.concatenate([own_acc, jnp.zeros((8, CELLS), F32)], axis=0)
    acc = jnp.concatenate([acc + own_acc, jnp.zeros((CELLS - 24, CELLS), F32)], axis=0)
    sums = lax.dot_general(
        jnp.ones((8, CELLS), F32),
        acc,
        (((1,), (1,)), ((), ())),
        precision=lax.Precision.HIGHEST,
        preferred_element_type=F32,
    )
    parts = three_parts(sums[0:1])
    out_dev[:, 16:32, :] = (tail_dev[...] + parts[None]).astype(BF16)
    out_lev[:, 16:32, :] = tail_lev[...].astype(BF16)


def relay_kernel(recv, tail, send_in, send_out, new_tail, sem):
    del send_in
    total = sum_parts(jnp.sum(recv[:, 16:32, :].astype(F32), axis=0))
    new_tail[...] = (tail[...] + three_parts(total)[None]).astype(BF16)
    copy = pltpu.make_async_copy(new_tail, send_out.at[:, pl.ds(16, 16), :], sem)
    copy.start()
    copy.wait()


def placed(recv):
    peers = recv.shape[0]
    row = lax.broadcasted_iota(jnp.int32, (COMP * BLK, CELLS), 0).astype(F32)
    total = jnp.zeros((COMP * BLK, CELLS), F32)
    for g in range(peers // GROUP):
        sl = slice(g * GROUP, (g + 1) * GROUP)
        codes = jnp.sum(recv[sl, 16:32, :].astype(F32), axis=0)[8:9]
        pick = jnp.where(row == codes, 1.0, 0.0).astype(BF16)
        data = recv[sl].reshape(GROUP * ROWS, CELLS)
        total = total + jnp.dot(pick, data, preferred_element_type=F32)
    return total


def intra_kernel(recv, own, out):
    out[...] = own[...] + placed(recv)


def final_kernel(recv, base, out, totals):
    out[...] = base[...] + placed(recv)
    total = sum_parts(jnp.sum(recv[:, 16:32, :].astype(F32), axis=0))
    both = jnp.broadcast_to(total, (8, CELLS))
    both = both + pltpu.roll(both, CELLS - COMP, 1)
    totals[...] = both[0:1, 0:COMP] * (1.0 / (CELLS * BLK))


def body(
    fields,
    own_src,
    own_weight,
    send_block,
    send_target,
    send_count,
    send_weight,
    left_block,
    left_target,
    left_count,
    left_weight,
):
    peers = send_weight.shape[2]
    levels = left_weight.shape[2]
    rows = COMP * BLK
    flat = jnp.transpose(fields[0], (1, 0, 2)).reshape(rows, CELLS)
    place = jnp.stack([lax.axis_index(DEV), lax.axis_index("level")]).astype(jnp.int32)
    anywhere = pl.BlockSpec(memory_space=pl.ANY)
    vmem = pl.BlockSpec(memory_space=pltpu.VMEM)
    smem = pl.BlockSpec(memory_space=pltpu.SMEM)
    send_dev, send_lev, tail_lev, own = pl.pallas_call(
        terms_kernel,
        name="terms",
        in_specs=[smem] + [anywhere] * 11,
        out_specs=[vmem] * 4,
        out_shape=[
            jax.ShapeDtypeStruct((peers, ROWS, CELLS), BF16),
            jax.ShapeDtypeStruct((levels, ROWS, CELLS), BF16),
            jax.ShapeDtypeStruct((levels, 16, CELLS), F32),
            jax.ShapeDtypeStruct((rows, CELLS), F32),
        ],
        scratch_shapes=[
            pltpu.VMEM((rows, CELLS), F32),
            pltpu.VMEM((BLK + 1, ROWS, CELLS), F32),
            pltpu.VMEM((BLK + 1, ROWS, CELLS), F32),
            pltpu.VMEM((BLK + 1, ROWS, CELLS), BF16),
            pltpu.VMEM((BLK + 1, ROWS, CELLS), BF16),
            pltpu.VMEM((peers, CAP * CELLS, CELLS), BF16),
            pltpu.VMEM((levels, CAP * CELLS, CELLS), BF16),
            pltpu.VMEM((BLK, CELLS, CELLS), BF16),
            pltpu.VMEM((peers, 16, CELLS), F32),
            pltpu.SMEM((1, BLK), jnp.int32),
            pltpu.SMEM((CAP, peers), jnp.int32),
            pltpu.SMEM((CAP, peers), jnp.int32),
            pltpu.SMEM((1, peers), jnp.int32),
            pltpu.SMEM((CAP, levels), jnp.int32),
            pltpu.SMEM((CAP, levels), jnp.int32),
            pltpu.SMEM((1, levels), jnp.int32),
            pltpu.SemaphoreType.DMA((8,)),
            pltpu.SemaphoreType.DMA((W_CHUNKS + 2,)),
        ],
    )(
        place,
        flat,
        own_src,
        own_weight[0],
        send_block[0, 0].T,
        send_target[0, 0].T,
        send_count[0],
        send_weight.reshape(peers, CAP * CELLS, CELLS),
        left_block[0, 0].T,
        left_target[0, 0].T,
        left_count[0],
        left_weight.reshape(levels, CAP * CELLS, CELLS),
    )
    got_dev = lax.all_to_all(send_dev, DEV, split_axis=0, concat_axis=0, tiled=True)
    send_lev = pl.pallas_call(
        relay_kernel,
        name="relay",
        in_specs=[vmem, vmem, anywhere],
        out_specs=anywhere,
        out_shape=jax.ShapeDtypeStruct(send_lev.shape, BF16),
        scratch_shapes=[pltpu.VMEM((levels, 16, CELLS), BF16), pltpu.SemaphoreType.DMA],
        input_output_aliases={2: 0},
    )(got_dev, tail_lev, send_lev)
    got_lev = lax.all_to_all(send_lev, "level", split_axis=0, concat_axis=0, tiled=True)
    base = pl.pallas_call(
        intra_kernel,
        name="intra",
        in_specs=[vmem, vmem],
        out_specs=vmem,
        out_shape=jax.ShapeDtypeStruct((rows, CELLS), F32),
    )(got_dev, own)
    remapped, totals = pl.pallas_call(
        final_kernel,
        name="final",
        in_specs=[vmem, vmem],
        out_specs=[vmem, vmem],
        out_shape=[
            jax.ShapeDtypeStruct((rows, CELLS), F32),
            jax.ShapeDtypeStruct((1, COMP), F32),
        ],
    )(got_lev, base)
    remapped = jnp.transpose(remapped.reshape(COMP, BLK, CELLS), (1, 0, 2))
    return (remapped[None], totals.reshape(COMP))


def solution(mesh):
    split = Mesh(
        mesh.devices.reshape(mesh.shape["level"], 4, 4, 2), ("level", "dev_0", "dev_1", "dev_2")
    )
    return jax.shard_map(
        body,
        mesh=split,
        in_specs=(
            P("level", DEV, None, None),
            P("level", DEV),
            P("level", DEV, None, None),
            P("level", DEV, None, None),
            P("level", DEV, None, None),
            P("level", DEV, None),
            P("level", DEV, None, None, None, None),
            P("level", DEV, None, None),
            P("level", DEV, None, None),
            P("level", DEV, None),
            P("level", DEV, None, None, None, None),
        ),
        out_specs=(P("level", DEV, None, None), P()),
        check_vma=False,
    )
```

time: 133 us -> 55.5 us (0.42)
  blocking collectives: 51.6 us -> 20.1 us
  starting transfers between devices: 36.1 us -> 12.4 us
  waiting for transfers between devices: 23 us -> 10.2 us
  Pallas kernels: 0 us -> 9.64 us
  local copies, waits for them, and re-layouts: 9.26 us -> 0.65 us
  other arithmetic: 7.24 us -> 0.59 us
  matrix products: 4.41 us -> 0 us
    psum x4 -> x0, blocking collectives: 51.6 us -> none  [one_axis_at_a_time(): shard = lax.psum(shard, axis)]
    all_to_all x4 -> x1, starting transfers between devices: 36.1 us -> 12.4 us  [body(): lax.all_to_all(send_lev, 'level', split_axis=0, concat_axis=0, tiled=True)]
    all_to_all x0 -> x1, blocking collectives: none -> 20.1 us  [body(): lax.all_to_all(send_dev, DEV, split_axis=0, concat_axis=0, tiled=True)]
    all_to_all x4 -> x1, waiting for transfers between devices: 23 us -> 10.2 us  [body(): lax.all_to_all(send_lev, 'level', split_axis=0, concat_axis=0, tiled=True)]
    pallas_call x0 -> x4, Pallas kernels: none -> 9.64 us  [the longest x1 4.29 us: body(): pl.pallas_call(terms_kernel, name='terms', in_specs=[smem] + [anywhere] *...]
    dot_general x5 -> x0, matrix products: 4.41 us -> none  [the longest x2 2.74 us: apply_weights(): jnp.einsum('pcmk,pcki->pcmi', donors, weights, preferred_element_type=jnp...]
    all_to_all x5 -> x0, local copies, waits for them, and re-layouts: 2.94 us -> none  [the longest x1 1.51 us: body(): lax.all_to_all(send_target[0, 0], DEV, split_axis=0, concat_axis=0, tiled...]
    gather x3 -> x0, local copies, waits for them, and re-layouts: 2.6 us -> none  [the longest x2 2.02 us: pick_donors(): donors = rounded[block_index]]
  transfers between devices with their start and end apart: 4 -> 1, of which waited for: 3 -> 1; matrix products, arithmetic and copies ran while one was open for 13% -> 0% of each run, Pallas kernels for 0% -> 3%
where the time goes in v1:
time: 55.5 us; the launch traced here: 54.4 us
  blocking collectives  20.1 us (36%)
  starting transfers between devices  12.4 us (22%)
  waiting for transfers between devices  10.2 us (18%)
  Pallas kernels  9.64 us (17%)
  between operations  0.66 us (1%)
  local copies, waits for them, and re-layouts  0.65 us (1%)
  other arithmetic  0.59 us (1%)
    all_to_all x1, blocking collectives, body(): lax.all_to_all(send_dev, DEV, split_axis=0, concat_axis=0, tiled=True)  20.1 us
    all_to_all x1, starting transfers between devices, body(): lax.all_to_all(send_lev, 'level', split_axis=0, concat_axis=0, tiled=True)  12.4 us
    all_to_all x1, waiting for transfers between devices, body(): lax.all_to_all(send_lev, 'level', split_axis=0, concat_axis=0, tiled=True)  10.2 us
    pallas_call x1, Pallas kernels, body(): pl.pallas_call(terms_kernel, name='terms', in_specs=[smem] + [anywhere] *...  4.29 us
    pallas_call x1, Pallas kernels, body(): pl.pallas_call(intra_kernel, name='intra', in_specs=[vmem, vmem], out_spe...  1.88 us
    pallas_call x1, Pallas kernels, body(): pl.pallas_call(final_kernel, name='final', in_specs=[vmem, vmem], out_spe...  1.8 us
    pallas_call x1, Pallas kernels, body(): pl.pallas_call(relay_kernel, name='relay', in_specs=[vmem, vmem, anywhere...  1.67 us
  transfers between devices with their start and end apart: 1, of which 1 were waited for; matrix products, arithmetic and copies ran while one was open for 0% of the time, Pallas kernels for 3%

profile of v1, /device:TPU:1, one launch (start us, length us, event | category | flops | bytes accessed | tf_op | source)
XLA Modules:
  0.0 54.4 jit_solution(17229790600779097410)
XLA Ops:
  0.6 0.6 %pad_add_fusion.place = s32[2]{0:T(128)} fusion(s32[1]{0:T(128)} %bitcast.1, s32[1]{0:T(128)} %bitcast), kind=kLoop, calls=%fused_computation | loop fusion | flops 2 | bytes 16 | tf_op jit(solution)/shard_map/stack | solution.py:227
  1.2 4.3 %terms.1 = (bf16[32,32,128]{2,1,0:T(8,128)(2,1)}, bf16[16,32,128]{2,1,0:T(8,128)(2,1)}, f32[16,16,128]{2,1,0:T(8,128)}, f32[192,128]{1,0:T(8,128)}) custom-call(s32[2]{0:T(128)} %pad_add_fusion.place, f32[192,128]{1,0:T(8,128)} %bitcast.33, s32[1,16]{1,0:T(1,128)} %own_src.1, bf16[16,128,128]{2,1,0:T(8,128)(2,1)} %bitcast.32, s32[2,32]{1,0:T(2,128)} %bitcast.34, ...), custom_call_target="tpu_custom_call" | custom-call | tf_op jit(solution)/shard_map/terms/pallas_call | solution.py:231
  5.5 20.1 %all_to_all.10.recv = bf16[32,32,128]{2,1,0:T(8,128)(2,1)} all-to-all(bf16[32,32,128]{2,1,0:T(8,128)(2,1)} %get-tuple-element.8), channel_id=1, replica_groups=mesh['level'=16,'dev_0'=4,'dev_1'=4,'dev_2'=2] {'dev_0','dev_1','dev_2'}, dimensions={0} | all-to-all | bytes 524288 | tf_op jit(solution)/shard_map/all_to_all | solution.py:276
  25.7 1.7 %relay.1 = bf16[16,32,128]{2,1,0:T(8,128)(2,1)} custom-call(bf16[32,32,128]{2,1,0:T(8,128)(2,1)} %all_to_all.10.recv, f32[16,16,128]{2,1,0:T(8,128)} %get-tuple-element.9.tail, bf16[16,32,128]{2,1,0:T(8,128)(2,1)} %get-tuple-element.10.send_in), custom_call_target="tpu_custom_call", output_to_operand_aliasing={{}: (2, {})} | custom-call | tf_op jit(solution)/shard_map/relay/pallas_call | solution.py:277
  27.4 12.4 %all-to-all-start.1 = ((bf16[16,32,128]{2,1,0:T(8,128)(2,1)}), bf16[16,32,128]{2,1,0:T(8,128)(2,1)S(1)}, u32[]{:S(2)}, u32[]{:S(2)}) async-start(bf16[16,32,128]{2,1,0:T(8,128)(2,1)} %relay.1), calls=%async_computation.1 | async-start | bytes 262144 | tf_op jit(solution)/shard_map/all_to_all | solution.py:286
  39.8 1.9 %intra.1.base = f32[192,128]{1,0:T(8,128)} custom-call(bf16[32,32,128]{2,1,0:T(8,128)(2,1)} %all_to_all.10.recv, f32[192,128]{1,0:T(8,128)} %get-tuple-element.11.own), custom_call_target="tpu_custom_call" | custom-call | tf_op jit(solution)/shard_map/intra/pallas_call | solution.py:287
  41.7 10.2 %all-to-all-done.1.recv = bf16[16,32,128]{2,1,0:T(8,128)(2,1)S(1)} async-done(((bf16[16,32,128]{2,1,0:T(8,128)(2,1)}), bf16[16,32,128]{2,1,0:T(8,128)(2,1)S(1)}, u32[]{:S(2)}, u32[]{:S(2)}) %all-to-all-start.1) | async-done | bytes 131104 | tf_op jit(solution)/shard_map/all_to_all | solution.py:286
  51.9 0.0 copy-start
  51.9 0.7 %copy-done = bf16[16,32,128]{2,1,0:T(8,128)(2,1)} copy-done((bf16[16,32,128]{2,1,0:T(8,128)(2,1)}, bf16[16,32,128]{2,1,0:T(8,128)(2,1)S(1)}, u32[]{:S(2)}) %copy-start) | copy-done | bytes 131096
  52.6 1.8 %final.1 = (f32[192,128]{1,0:T(8,128)}, f32[1,12]{1,0:T(1,128)}) custom-call(bf16[16,32,128]{2,1,0:T(8,128)(2,1)} %copy-done, f32[192,128]{1,0:T(8,128)} %intra.1.base), custom_call_target="tpu_custom_call" | custom-call | tf_op jit(solution)/shard_map/final/pallas_call | solution.py:294
Async XLA Ops:
  27.4 24.6 %all-to-all-start.1 = ((bf16[16,32,128]{2,1,0:T(8,128)(2,1)}), bf16[16,32,128]{2,1,0:T(8,128)(2,1)S(1)}, u32[]{:S(2)}, u32[]{:S(2)}) async-start(bf16[16,32,128]{2,1,0:T(8,128)(2,1)} %relay.1), calls=%async_computation.1 | async-start | bytes 262144 | tf_op jit(solution)/shard_map/all_to_all | solution.py:286
  51.9 0.7 %copy-start = (bf16[16,32,128]{2,1,0:T(8,128)(2,1)}, bf16[16,32,128]{2,1,0:T(8,128)(2,1)S(1)}, u32[]{:S(2)}) copy-start(bf16[16,32,128]{2,1,0:T(8,128)(2,1)S(1)} %all-to-all-done.1.recv) | copy-start | bytes 393220

commit v2 on v1

v2 whole, which is shorter than its diff:
```python
import jax
import jax.numpy as jnp
from jax import lax
from jax.experimental import pallas as pl
from jax.experimental.pallas import tpu as pltpu
from jax.sharding import PartitionSpec as P

START = {"dev": 31, "level": 12}
ORDER = ("dev", "level")
COMP = 12
CELLS = 128
BLK = 16
CAP = 2
ROWS = 32
GROUP = CELLS // ROWS
W_CHUNKS = 4
F32 = jnp.float32
BF16 = jnp.bfloat16


def code_tile(t0, t1, slot):
    row = lax.broadcasted_iota(jnp.int32, (8, CELLS), 0)
    lane = lax.broadcasted_iota(jnp.int32, (8, CELLS), 1)
    r = lane % ROWS
    here = (row == 0) & (lane // ROWS == slot)
    second = r >= COMP
    comp = jnp.where(second, r - COMP, r)
    code = comp * BLK + jnp.where(second, t1, t0)
    code = jnp.where(r < CAP * COMP, code, 255)
    return jnp.where(here, code, 0).astype(F32)


def three_parts(total):
    row = lax.broadcasted_iota(jnp.int32, (16, CELLS), 0)
    full = jnp.broadcast_to(total, (16, CELLS))
    hi = full.astype(BF16).astype(F32)
    mid = (full - hi).astype(BF16).astype(F32)
    low = full - hi - mid
    zero = jnp.zeros_like(full)
    return jnp.where(row == 9, hi, jnp.where(row == 10, mid, jnp.where(row == 11, low, zero)))


def sum_parts(tail):
    return tail[9:10] + tail[10:11] + tail[11:12]


def terms_kernel(
    fields,
    own_src,
    own_w,
    send_blk,
    send_tgt,
    send_cnt,
    send_w,
    left_blk,
    left_tgt,
    left_cnt,
    left_w,
    out_dev,
    out_lev,
    own_out,
    fld,
    first32,
    second32,
    first,
    second,
    wd,
    wl,
    wo,
    s_src,
    s_sblk,
    s_stgt,
    s_scnt,
    s_lblk,
    s_ltgt,
    s_lcnt,
    sems,
    wsems,
):
    peers = send_w.shape[0]
    levels = left_w.shape[0]
    small = []
    pairs = (
        (fields, fld),
        (own_src, s_src),
        (send_blk, s_sblk),
        (send_tgt, s_stgt),
        (send_cnt, s_scnt),
        (left_blk, s_lblk),
        (left_tgt, s_ltgt),
        (left_cnt, s_lcnt),
    )
    for n, (src, dst) in enumerate(pairs):
        copy = pltpu.make_async_copy(src, dst, sems.at[n])
        copy.start()
        small.append(copy)
    step = peers // W_CHUNKS
    weights = []
    for n in range(W_CHUNKS):
        sl = pl.ds(n * step, step)
        copy = pltpu.make_async_copy(send_w.at[sl], wd.at[sl], wsems.at[n])
        copy.start()
        weights.append(copy)
    left_copy = pltpu.make_async_copy(left_w, wl, wsems.at[W_CHUNKS])
    left_copy.start()
    own_copy = pltpu.make_async_copy(own_w, wo, wsems.at[W_CHUNKS + 1])
    own_copy.start()

    first32[...] = jnp.zeros(first32.shape, F32)
    second32[...] = jnp.zeros(second32.shape, F32)
    small[0].wait()
    for b in range(BLK):
        one = fld[pl.ds(b, COMP, stride=BLK), :]
        first32[b, 0:COMP, :] = one
        second32[b, COMP : 2 * COMP, :] = one
    first[...] = first32[...].astype(BF16)
    second[...] = second32[...].astype(BF16)
    for copy in small[1:]:
        copy.wait()

    def group_terms(out, blk, tgt, cnt, weight, axis):
        size = out.shape[0]
        place = lax.rem(lax.axis_index(axis) + (size - START[axis]), size)
        slot = lax.rem(place, GROUP)

        def one(n, acc):
            live = cnt[0, n]
            b0 = jnp.where(live > 0, blk[0, n], BLK)
            b1 = jnp.where(live > 1, blk[1, n], BLK)
            lhs = jnp.concatenate([first[b0], second[b1]], axis=1)
            t = jnp.dot(lhs, weight[n], preferred_element_type=F32)
            to = lax.rem(n + (size - START[axis]), size)
            out[to, 0:16, :] = t[0:16].astype(BF16)
            tail = jnp.concatenate([t[16:24], code_tile(tgt[0, n], tgt[1, n], slot)], axis=0)
            out[to, 16:32, :] = tail.astype(BF16)
            return acc + t[0:24]

        return one

    dev_step = group_terms(out_dev, s_sblk, s_stgt, s_scnt, wd, "dev")
    lev_step = group_terms(out_lev, s_lblk, s_ltgt, s_lcnt, wl, "level")
    acc = jnp.zeros((24, CELLS), F32)
    for n in range(W_CHUNKS):
        weights[n].wait()
        acc = lax.fori_loop(n * step, (n + 1) * step, dev_step, acc, unroll=True)
    left_copy.wait()
    acc = lax.fori_loop(0, levels, lev_step, acc, unroll=True)
    own_copy.wait()
    own_acc = jnp.zeros((16, CELLS), F32)
    for b in range(BLK):
        t = jnp.dot(first[s_src[0, b], 0:16, :], wo[b], preferred_element_type=F32)
        own_out[pl.ds(b, COMP, stride=BLK), :] = t[0:COMP]
        own_acc = own_acc + t
    own_acc = jnp.concatenate([own_acc, jnp.zeros((8, CELLS), F32)], axis=0)
    acc = jnp.concatenate([acc + own_acc, jnp.zeros((CELLS - 24, CELLS), F32)], axis=0)
    sums = lax.dot_general(
        jnp.ones((8, CELLS), F32),
        acc,
        (((1,), (1,)), ((), ())),
        precision=lax.Precision.HIGHEST,
        preferred_element_type=F32,
    )
    add_parts(out_dev if ORDER[0] == "dev" else out_lev, sums[0:1])


def add_parts(message, total):
    tail = message[:, 16:32, :].astype(F32)
    message[:, 16:32, :] = (tail + three_parts(total)[None]).astype(BF16)


def relay_kernel(recv, send_in, send_out):
    del send_in
    add_parts(send_out, sum_parts(jnp.sum(recv[:, 16:32, :].astype(F32), axis=0)))


def placed(recv):
    peers = recv.shape[0]
    row = lax.broadcasted_iota(jnp.int32, (COMP * BLK, CELLS), 0).astype(F32)
    total = jnp.zeros((COMP * BLK, CELLS), F32)
    for g in range(peers // GROUP):
        sl = slice(g * GROUP, (g + 1) * GROUP)
        codes = jnp.sum(recv[sl, 16:32, :].astype(F32), axis=0)[8:9]
        pick = jnp.where(row == codes, 1.0, 0.0).astype(BF16)
        data = recv[sl].reshape(GROUP * ROWS, CELLS)
        total = total + jnp.dot(pick, data, preferred_element_type=F32)
    return total


def final_kernel(early, late, own, out, totals):
    out[...] = own[...] + placed(early) + placed(late)
    total = sum_parts(jnp.sum(late[:, 16:32, :].astype(F32), axis=0))
    both = jnp.broadcast_to(total, (8, CELLS))
    both = both + pltpu.roll(both, CELLS - COMP, 1)
    totals[...] = both[0:1, 0:COMP] * (1.0 / (CELLS * BLK))


def in_vmem(x):
    return pltpu.with_memory_space_constraint(x, pltpu.VMEM)


def exchange(message, axis):
    size = message.shape[0]
    groups = [[(START[axis] + n) % size for n in range(size)]]
    got = lax.all_to_all(
        in_vmem(message), axis, 0, 0, axis_index_groups=groups, tiled=True
    )
    return in_vmem(got)


def body(
    fields,
    own_src,
    own_weight,
    send_block,
    send_target,
    send_count,
    send_weight,
    left_block,
    left_target,
    left_count,
    left_weight,
):
    peers = send_weight.shape[2]
    levels = left_weight.shape[2]
    rows = COMP * BLK
    flat = jnp.transpose(fields[0], (1, 0, 2)).reshape(rows, CELLS)
    anywhere = pl.BlockSpec(memory_space=pl.ANY)
    vmem = pl.BlockSpec(memory_space=pltpu.VMEM)
    send_dev, send_lev, own = pl.pallas_call(
        terms_kernel,
        name="terms",
        in_specs=[anywhere] * 11,
        out_specs=[vmem] * 3,
        out_shape=[
            pltpu.VMEM((peers, ROWS, CELLS), BF16),
            pltpu.VMEM((levels, ROWS, CELLS), BF16),
            pltpu.VMEM((rows, CELLS), F32),
        ],
        scratch_shapes=[
            pltpu.VMEM((rows, CELLS), F32),
            pltpu.VMEM((BLK + 1, ROWS, CELLS), F32),
            pltpu.VMEM((BLK + 1, ROWS, CELLS), F32),
            pltpu.VMEM((BLK + 1, ROWS, CELLS), BF16),
            pltpu.VMEM((BLK + 1, ROWS, CELLS), BF16),
            pltpu.VMEM((peers, CAP * CELLS, CELLS), BF16),
            pltpu.VMEM((levels, CAP * CELLS, CELLS), BF16),
            pltpu.VMEM((BLK, CELLS, CELLS), BF16),
            pltpu.SMEM((1, BLK), jnp.int32),
            pltpu.SMEM((CAP, peers), jnp.int32),
            pltpu.SMEM((CAP, peers), jnp.int32),
            pltpu.SMEM((1, peers), jnp.int32),
            pltpu.SMEM((CAP, levels), jnp.int32),
            pltpu.SMEM((CAP, levels), jnp.int32),
            pltpu.SMEM((1, levels), jnp.int32),
            pltpu.SemaphoreType.DMA((8,)),
            pltpu.SemaphoreType.DMA((W_CHUNKS + 2,)),
        ],
    )(
        flat,
        own_src,
        own_weight[0],
        send_block[0, 0].T,
        send_target[0, 0].T,
        send_count[0],
        send_weight.reshape(peers, CAP * CELLS, CELLS),
        left_block[0, 0].T,
        left_target[0, 0].T,
        left_count[0],
        left_weight.reshape(levels, CAP * CELLS, CELLS),
    )
    sends = {"dev": send_dev, "level": send_lev}
    early = exchange(sends[ORDER[0]], ORDER[0])
    second = sends[ORDER[1]]
    second = pl.pallas_call(
        relay_kernel,
        name="relay",
        in_specs=[vmem, vmem],
        out_specs=vmem,
        out_shape=pltpu.VMEM(second.shape, BF16),
        input_output_aliases={1: 0},
    )(early, in_vmem(second))
    late = exchange(second, ORDER[1])
    remapped, totals = pl.pallas_call(
        final_kernel,
        name="final",
        in_specs=[vmem, vmem, vmem],
        out_specs=[vmem, vmem],
        out_shape=[
            jax.ShapeDtypeStruct((rows, CELLS), F32),
            jax.ShapeDtypeStruct((1, COMP), F32),
        ],
    )(early, late, in_vmem(own))
    remapped = jnp.transpose(remapped.reshape(COMP, BLK, CELLS), (1, 0, 2))
    return (remapped[None], totals.reshape(COMP))


def solution(mesh):
    return jax.shard_map(
        body,
        mesh=mesh,
        in_specs=(
            P("level", "dev", None, None),
            P("level", "dev"),
            P("level", "dev", None, None),
            P("level", "dev", None, None),
            P("level", "dev", None, None),
            P("level", "dev", None),
            P("level", "dev", None, None, None, None),
            P("level", "dev", None, None),
            P("level", "dev", None, None),
            P("level", "dev", None),
            P("level", "dev", None, None, None, None),
        ),
        out_specs=(P("level", "dev", None, None), P()),
        check_vma=False,
    )
```

time: 55.5 us -> 44.7 us (0.81); the launches traced: 54.4 us -> 44.5 us
  blocking collectives: 20.1 us -> 40 us
  starting transfers between devices: 12.4 us -> 0 us
  waiting for transfers between devices: 10.2 us -> 0 us
  Pallas kernels: 9.64 us -> 3.81 us
  local copies, waits for them, and re-layouts: 0.65 us -> 0 us
  other arithmetic: 0.59 us -> 0 us
    all_to_all x1 -> x2, blocking collectives: 20.1 us -> 40 us  [exchange(): lax.all_to_all(in_vmem(message), axis, 0, 0, axis_index_groups=groups, ti...]
    all_to_all x1 -> x0, starting transfers between devices: 12.4 us -> none  [body(): lax.all_to_all(send_lev, 'level', split_axis=0, concat_axis=0, tiled=True)]
    all_to_all x1 -> x0, waiting for transfers between devices: 10.2 us -> none  [body(): lax.all_to_all(send_lev, 'level', split_axis=0, concat_axis=0, tiled=True)]
    pallas_call x4 -> x3, Pallas kernels: 9.64 us -> 3.81 us  [the longest x1 2.81 us: body(): pl.pallas_call(terms_kernel, name='terms', in_specs=[anywhere] * 11, out_...]
    unnamed x2 -> x0, local copies, waits for them, and re-layouts: 0.65 us -> none
    another operation x1 -> x0, other arithmetic: 0.59 us -> none  [body(): jnp.stack([lax.axis_index(DEV), lax.axis_index('level')]).astype(jnp.int32)]
  transfers between devices with their start and end apart: 1 -> 0, of which waited for: 1 -> 0; matrix products, arithmetic and copies ran while one was open for 0% -> 0% of each run, Pallas kernels for 3% -> 0%
where the time goes in v2:
time: 44.7 us; the launch traced here: 44.5 us
  blocking collectives  40 us (89%)
  Pallas kernels  3.81 us (9%)
  between operations  0.65 us (1%)
    all_to_all x2, blocking collectives, exchange(): lax.all_to_all(in_vmem(message), axis, 0, 0, axis_index_groups=groups, ti...  40 us
    pallas_call x1, Pallas kernels, body(): pl.pallas_call(terms_kernel, name='terms', in_specs=[anywhere] * 11, out_...  2.81 us
    pallas_call x1, Pallas kernels, body(): pl.pallas_call(final_kernel, name='final', in_specs=[vmem, vmem, vmem], o...  0.95 us

profile of v2, /device:TPU:1, one launch (start us, length us, event | category | flops | bytes accessed | tf_op | source)
XLA Modules:
  0.0 44.5 jit_solution(16718874986134184890)
XLA Ops:
  0.6 2.8 %terms.1 = (bf16[32,32,128]{2,1,0:T(8,128)(2,1)S(1)}, bf16[16,32,128]{2,1,0:T(8,128)(2,1)S(1)}, f32[192,128]{1,0:T(8,128)S(1)}) custom-call(f32[192,128]{1,0:T(8,128)} %bitcast.31, s32[1,16]{1,0:T(1,128)} %own_src.1, bf16[16,128,128]{2,1,0:T(8,128)(2,1)} %bitcast.30, s32[2,32]{1,0:T(2,128)} %bitcast.32, s32[2,32]{1,0:T(2,128)} %bitcast.33, ...), custom_call_target="tpu_custom_call" | custom-call | tf_op jit(solution)/shard_map/terms/pallas_call | solution.py:229
  3.4 18.5 %all_to_all.10.recv.early = bf16[32,32,128]{2,1,0:T(8,128)(2,1)S(1)} all-to-all(bf16[32,32,128]{2,1,0:T(8,128)(2,1)S(1)} %get-tuple-element.7), channel_id=1, replica_groups={{31,0,1,2,3,4,5,6,7,8,9,10,11,12,13,14,15,16,17,18,19,20,21,22,23,24,25..., dimensions={0} | all-to-all | bytes 524288 | tf_op jit(solution)/shard_map/all_to_all | solution.py:204
  22.0 0.1 relay.1
  22.0 21.5 %all_to_all.11.late = bf16[16,32,128]{2,1,0:T(8,128)(2,1)S(1)} all-to-all(bf16[16,32,128]{2,1,0:T(8,128)(2,1)S(1)} %relay.1), channel_id=1, replica_groups={{384,416,448,480,0,32,64,96,128,160,192,224,256,288,320,352},{385,417,4..., dimensions={0} | all-to-all | bytes 262144 | tf_op jit(solution)/shard_map/all_to_all | solution.py:204
  43.5 1.0 %final.1 = (f32[192,128]{1,0:T(8,128)}, f32[1,12]{1,0:T(1,128)}) custom-call(bf16[32,32,128]{2,1,0:T(8,128)(2,1)S(1)} %all_to_all.10.recv.early, bf16[16,32,128]{2,1,0:T(8,128)(2,1)S(1)} %all_to_all.11.late, f32[192,128]{1,0:T(8,128)S(1)} %get-tuple-element.9.own), custom_call_target="tpu_custom_call" | custom-call | tf_op jit(solution)/shard_map/final/pallas_call | solution.py:283

commit v3 on v2

--- a/solution.py
+++ b/solution.py
@@ -5,14 +5,19 @@
 from jax.experimental.pallas import tpu as pltpu
 from jax.sharding import PartitionSpec as P
 
-START = {"dev": 31, "level": 12}
+GROUPS = {
+    "dev": [21, 22, 23, 24, 25, 26, 27, 28, 29, 30, 31, 0, 1, 2, 3, 4, 5, 6, 7, 8, 9, 10, 11, 12, 13, 14, 15, 16, 17, 18, 19, 20],
+    "level": [10, 0, 1, 2, 3, 15, 4, 14, 5, 13, 6, 12, 7, 11, 8, 9],
+}
 ORDER = ("dev", "level")
 COMP = 12
 CELLS = 128
 BLK = 16
 CAP = 2
-ROWS = 32
-GROUP = CELLS // ROWS
+ROWS = 26
+PAIRS = ROWS // 2
+GROUP = 4
+PART = 32
 W_CHUNKS = 4
 F32 = jnp.float32
 BF16 = jnp.bfloat16
@@ -20,9 +25,8 @@
 
 def code_tile(t0, t1, slot):
     row = lax.broadcasted_iota(jnp.int32, (8, CELLS), 0)
-    lane = lax.broadcasted_iota(jnp.int32, (8, CELLS), 1)
-    r = lane % ROWS
-    here = (row == 0) & (lane // ROWS == slot)
+    r = lax.broadcasted_iota(jnp.int32, (8, CELLS), 1) - slot * ROWS
+    here = (row == 0) & (r >= 0) & (r < ROWS)
     second = r >= COMP
     comp = jnp.where(second, r - COMP, r)
     code = comp * BLK + jnp.where(second, t1, t0)
@@ -31,17 +35,24 @@
 
 
 def three_parts(total):
-    row = lax.broadcasted_iota(jnp.int32, (16, CELLS), 0)
-    full = jnp.broadcast_to(total, (16, CELLS))
+    row = lax.broadcasted_iota(jnp.int32, (8, CELLS), 0)
+    full = jnp.broadcast_to(total, (8, CELLS))
     hi = full.astype(BF16).astype(F32)
     mid = (full - hi).astype(BF16).astype(F32)
     low = full - hi - mid
-    zero = jnp.zeros_like(full)
-    return jnp.where(row == 9, hi, jnp.where(row == 10, mid, jnp.where(row == 11, low, zero)))
-
-
-def sum_parts(tail):
-    return tail[9:10] + tail[10:11] + tail[11:12]
+    parts = hi + pltpu.roll(mid, PART, 1) + pltpu.roll(low, 2 * PART, 1)
+    return jnp.where(row == 1, parts, jnp.zeros_like(parts))
+
+
+def sum_parts(row):
+    full = jnp.broadcast_to(row, (8, CELLS))
+    full = full + pltpu.roll(full, CELLS - PART, 1) + pltpu.roll(full, CELLS - 2 * PART, 1)
+    lane = lax.broadcasted_iota(jnp.int32, (8, CELLS), 1)
+    return jnp.where(lane < CAP * COMP, full, jnp.zeros_like(full))
+
+
+def last_pair(recv, sl):
+    return jnp.sum(recv[sl, PAIRS - 1].astype(F32), axis=0)
 
 
 def terms_kernel(
@@ -90,10 +101,9 @@
         (left_tgt, s_ltgt),
         (left_cnt, s_lcnt),
     )
-    for n, (src, dst) in enumerate(pairs):
-        copy = pltpu.make_async_copy(src, dst, sems.at[n])
-        copy.start()
-        small.append(copy)
+    copy = pltpu.make_async_copy(fields, fld, sems.at[0])
+    copy.start()
+    small.append(copy)
     step = peers // W_CHUNKS
     weights = []
     for n in range(W_CHUNKS):
@@ -106,6 +116,10 @@
     own_copy = pltpu.make_async_copy(own_w, wo, wsems.at[W_CHUNKS + 1])
     own_copy.start()
 
+    for n, (src, dst) in enumerate(pairs[1:], 1):
+        copy = pltpu.make_async_copy(src, dst, sems.at[n])
+        copy.start()
+        small.append(copy)
     first32[...] = jnp.zeros(first32.shape, F32)
     second32[...] = jnp.zeros(second32.shape, F32)
     small[0].wait()
@@ -120,8 +134,10 @@
 
     def group_terms(out, blk, tgt, cnt, weight, axis):
         size = out.shape[0]
-        place = lax.rem(lax.axis_index(axis) + (size - START[axis]), size)
-        slot = lax.rem(place, GROUP)
+        here = lax.axis_index(axis)
+        slot = jnp.int32(0)
+        for n, member in enumerate(GROUPS[axis]):
+            slot = jnp.where(here == member, n % GROUP, slot)
 
         def one(n, acc):
             live = cnt[0, n]
@@ -129,10 +145,11 @@
             b1 = jnp.where(live > 1, blk[1, n], BLK)
             lhs = jnp.concatenate([first[b0], second[b1]], axis=1)
             t = jnp.dot(lhs, weight[n], preferred_element_type=F32)
-            to = lax.rem(n + (size - START[axis]), size)
-            out[to, 0:16, :] = t[0:16].astype(BF16)
-            tail = jnp.concatenate([t[16:24], code_tile(tgt[0, n], tgt[1, n], slot)], axis=0)
-            out[to, 16:32, :] = tail.astype(BF16)
+            to = GROUPS[axis].index(n)
+            flat = out.reshape(size * ROWS, CELLS)
+            codes = code_tile(tgt[0, n], tgt[1, n], slot)
+            message = jnp.concatenate([t[0:24], codes], axis=0).astype(BF16)
+            flat[to * ROWS : (to + 1) * ROWS, :] = message[0:ROWS]
             return acc + t[0:24]
 
         return one
@@ -142,9 +159,11 @@
     acc = jnp.zeros((24, CELLS), F32)
     for n in range(W_CHUNKS):
         weights[n].wait()
-        acc = lax.fori_loop(n * step, (n + 1) * step, dev_step, acc, unroll=True)
+        for peer in range(n * step, (n + 1) * step):
+            acc = dev_step(peer, acc)
     left_copy.wait()
-    acc = lax.fori_loop(0, levels, lev_step, acc, unroll=True)
+    for level in range(levels):
+        acc = lev_step(level, acc)
     own_copy.wait()
     own_acc = jnp.zeros((16, CELLS), F32)
     for b in range(BLK):
@@ -164,32 +183,31 @@
 
 
 def add_parts(message, total):
-    tail = message[:, 16:32, :].astype(F32)
-    message[:, 16:32, :] = (tail + three_parts(total)[None]).astype(BF16)
+    pair = message[:, PAIRS - 1].astype(F32) + three_parts(total)[0:2][None]
+    message[:, PAIRS - 1] = pair.astype(BF16)
 
 
 def relay_kernel(recv, send_in, send_out):
     del send_in
-    add_parts(send_out, sum_parts(jnp.sum(recv[:, 16:32, :].astype(F32), axis=0)))
+    add_parts(send_out, sum_parts(last_pair(recv, slice(None))[1:2])[0:1])
 
 
 def placed(recv):
     peers = recv.shape[0]
+    flat = recv.reshape(peers * ROWS, CELLS)
     row = lax.broadcasted_iota(jnp.int32, (COMP * BLK, CELLS), 0).astype(F32)
     total = jnp.zeros((COMP * BLK, CELLS), F32)
     for g in range(peers // GROUP):
-        sl = slice(g * GROUP, (g + 1) * GROUP)
-        codes = jnp.sum(recv[sl, 16:32, :].astype(F32), axis=0)[8:9]
-        pick = jnp.where(row == codes, 1.0, 0.0).astype(BF16)
-        data = recv[sl].reshape(GROUP * ROWS, CELLS)
+        codes = last_pair(recv, slice(g * GROUP, (g + 1) * GROUP))[0:1]
+        pick = jnp.where(row == codes, 1.0, 0.0).astype(BF16)[:, : GROUP * ROWS]
+        data = flat[g * GROUP * ROWS : (g + 1) * GROUP * ROWS, :]
         total = total + jnp.dot(pick, data, preferred_element_type=F32)
     return total
 
 
 def final_kernel(early, late, own, out, totals):
     out[...] = own[...] + placed(early) + placed(late)
-    total = sum_parts(jnp.sum(late[:, 16:32, :].astype(F32), axis=0))
-    both = jnp.broadcast_to(total, (8, CELLS))
+    both = sum_parts(last_pair(late, slice(None))[1:2])
     both = both + pltpu.roll(both, CELLS - COMP, 1)
     totals[...] = both[0:1, 0:COMP] * (1.0 / (CELLS * BLK))
 
@@ -199,11 +217,8 @@
 
 
 def exchange(message, axis):
-    size = message.shape[0]
-    groups = [[(START[axis] + n) % size for n in range(size)]]
-    got = lax.all_to_all(
-        in_vmem(message), axis, 0, 0, axis_index_groups=groups, tiled=True
-    )
+    groups = [GROUPS[axis]]
+    got = lax.all_to_all(in_vmem(message), axis, 0, 0, axis_index_groups=groups, tiled=True)
     return in_vmem(got)
 
 
@@ -232,16 +247,16 @@
         in_specs=[anywhere] * 11,
         out_specs=[vmem] * 3,
         out_shape=[
-            pltpu.VMEM((peers, ROWS, CELLS), BF16),
-            pltpu.VMEM((levels, ROWS, CELLS), BF16),
+            pltpu.VMEM((peers, PAIRS, 2, CELLS), BF16),
+            pltpu.VMEM((levels, PAIRS, 2, CELLS), BF16),
             pltpu.VMEM((rows, CELLS), F32),
         ],
         scratch_shapes=[
             pltpu.VMEM((rows, CELLS), F32),
-            pltpu.VMEM((BLK + 1, ROWS, CELLS), F32),
-            pltpu.VMEM((BLK + 1, ROWS, CELLS), F32),
-            pltpu.VMEM((BLK + 1, ROWS, CELLS), BF16),
-            pltpu.VMEM((BLK + 1, ROWS, CELLS), BF16),
+            pltpu.VMEM((BLK + 1, 32, CELLS), F32),
+            pltpu.VMEM((BLK + 1, 32, CELLS), F32),
+            pltpu.VMEM((BLK + 1, 32, CELLS), BF16),
+            pltpu.VMEM((BLK + 1, 32, CELLS), BF16),
             pltpu.VMEM((peers, CAP * CELLS, CELLS), BF16),
             pltpu.VMEM((levels, CAP * CELLS, CELLS), BF16),
             pltpu.VMEM((BLK, CELLS, CELLS), BF16),

time: 44.7 us -> 41 us (0.917)
  blocking collectives: 40 us -> 35.9 us
    all_to_all x2, blocking collectives: 40 us -> 35.9 us  [exchange(): lax.all_to_all(in_vmem(message), axis, 0, 0, axis_index_groups=groups, ti...]
where the time goes in v3:
time: 41 us; the launch traced here: 40.6 us
  blocking collectives  35.9 us (88%)
  Pallas kernels  4.14 us (10%)
  between operations  0.65 us (2%)
    all_to_all x2, blocking collectives, exchange(): lax.all_to_all(in_vmem(message), axis, 0, 0, axis_index_groups=groups, ti...  35.9 us
    pallas_call x1, Pallas kernels, body(): pl.pallas_call(terms_kernel, name='terms', in_specs=[anywhere] * 11, out_...  2.91 us
    pallas_call x1, Pallas kernels, body(): pl.pallas_call(final_kernel, name='final', in_specs=[vmem, vmem, vmem], o...  1.05 us

profile of v3, /device:TPU:1, one launch (start us, length us, event | category | flops | bytes accessed | tf_op | source)
XLA Modules:
  0.0 40.6 jit_solution(10175244001802067822)
XLA Ops:
  0.6 2.9 %terms.1 = (bf16[32,13,2,128]{3,2,1,0:T(2,128)(2,1)S(1)}, bf16[16,13,2,128]{3,2,1,0:T(2,128)(2,1)S(1)}, f32[192,128]{1,0:T(8,128)S(1)}) custom-call(f32[192,128]{1,0:T(8,128)} %bitcast.31, s32[1,16]{1,0:T(1,128)} %own_src.1, bf16[16,128,128]{2,1,0:T(8,128)(2,1)} %bitcast.30, s32[2,32]{1,0:T(2,128)} %bitcast.32, s32[2,32]{1,0:T(2,128)} %bitcast.33, ...), custom_call_target="tpu_custom_call" | custom-call | tf_op jit(solution)/shard_map/terms/pallas_call | solution.py:244
  3.5 16.9 %all_to_all.10.recv.early = bf16[32,13,2,128]{3,2,1,0:T(2,128)(2,1)S(1)} all-to-all(bf16[32,13,2,128]{3,2,1,0:T(2,128)(2,1)S(1)} %get-tuple-element.7), channel_id=1, replica_groups={{21,22,23,24,25,26,27,28,29,30,31,0,1,2,3,4,5,6,7,8,9,10,11,12,13,14,15..., dimensions={0} | all-to-all | bytes 425984 | tf_op jit(solution)/shard_map/all_to_all | solution.py:221
  20.4 0.2 relay.1
  20.6 19.0 %all_to_all.11.late = bf16[16,13,2,128]{3,2,1,0:T(2,128)(2,1)S(1)} all-to-all(bf16[16,13,2,128]{3,2,1,0:T(2,128)(2,1)S(1)} %relay.1), channel_id=1, replica_groups={{320,0,32,64,96,480,128,448,160,416,192,384,224,352,256,288},{321,1,33,..., dimensions={0} | all-to-all | bytes 212992 | tf_op jit(solution)/shard_map/all_to_all | solution.py:221
  39.6 1.0 %final.1 = (f32[192,128]{1,0:T(8,128)}, f32[1,12]{1,0:T(1,128)}) custom-call(bf16[32,13,2,128]{3,2,1,0:T(2,128)(2,1)S(1)} %all_to_all.10.recv.early, bf16[16,13,2,128]{3,2,1,0:T(2,128)(2,1)S(1)} %all_to_all.11.late, f32[192,128]{1,0:T(8,128)S(1)} %get-tuple-element.9.own), custom_call_target="tpu_custom_call" | custom-call | tf_op jit(solution)/shard_map/final/pallas_call | solution.py:298

commit v4 on v3

--- a/solution.py
+++ b/solution.py
@@ -1,3 +1,5 @@
+import functools
+
 import jax
 import jax.numpy as jnp
 from jax import lax
@@ -10,6 +12,7 @@
     "level": [10, 0, 1, 2, 3, 15, 4, 14, 5, 13, 6, 12, 7, 11, 8, 9],
 }
 ORDER = ("dev", "level")
+WAITING = 8
 COMP = 12
 CELLS = 128
 BLK = 16
@@ -18,7 +21,7 @@
 PAIRS = ROWS // 2
 GROUP = 4
 PART = 32
-W_CHUNKS = 4
+W_CHUNKS = 2
 F32 = jnp.float32
 BF16 = jnp.bfloat16
 
@@ -105,16 +108,16 @@
     copy.start()
     small.append(copy)
     step = peers // W_CHUNKS
+    left_copy = pltpu.make_async_copy(left_w, wl, wsems.at[W_CHUNKS])
+    left_copy.start()
+    own_copy = pltpu.make_async_copy(own_w, wo, wsems.at[W_CHUNKS + 1])
+    own_copy.start()
     weights = []
     for n in range(W_CHUNKS):
         sl = pl.ds(n * step, step)
         copy = pltpu.make_async_copy(send_w.at[sl], wd.at[sl], wsems.at[n])
         copy.start()
         weights.append(copy)
-    left_copy = pltpu.make_async_copy(left_w, wl, wsems.at[W_CHUNKS])
-    left_copy.start()
-    own_copy = pltpu.make_async_copy(own_w, wo, wsems.at[W_CHUNKS + 1])
-    own_copy.start()
 
     for n, (src, dst) in enumerate(pairs[1:], 1):
         copy = pltpu.make_async_copy(src, dst, sems.at[n])
@@ -157,19 +160,19 @@
     dev_step = group_terms(out_dev, s_sblk, s_stgt, s_scnt, wd, "dev")
     lev_step = group_terms(out_lev, s_lblk, s_ltgt, s_lcnt, wl, "level")
     acc = jnp.zeros((24, CELLS), F32)
-    for n in range(W_CHUNKS):
-        weights[n].wait()
-        for peer in range(n * step, (n + 1) * step):
-            acc = dev_step(peer, acc)
     left_copy.wait()
+    own_copy.wait()
     for level in range(levels):
         acc = lev_step(level, acc)
-    own_copy.wait()
     own_acc = jnp.zeros((16, CELLS), F32)
     for b in range(BLK):
         t = jnp.dot(first[s_src[0, b], 0:16, :], wo[b], preferred_element_type=F32)
         own_out[pl.ds(b, COMP, stride=BLK), :] = t[0:COMP]
         own_acc = own_acc + t
+    for n in range(W_CHUNKS):
+        weights[n].wait()
+        for peer in range(n * step, (n + 1) * step):
+            acc = dev_step(peer, acc)
     own_acc = jnp.concatenate([own_acc, jnp.zeros((8, CELLS), F32)], axis=0)
     acc = jnp.concatenate([acc + own_acc, jnp.zeros((CELLS - 24, CELLS), F32)], axis=0)
     sums = lax.dot_general(
@@ -182,14 +185,34 @@
     add_parts(out_dev if ORDER[0] == "dev" else out_lev, sums[0:1])
 
 
+def scoped_terms(*refs):
+    pl.run_scoped(
+        functools.partial(terms_kernel, *refs),
+        pltpu.SemaphoreType.DMA((8,)),
+        pltpu.SemaphoreType.DMA((W_CHUNKS + 2,)),
+    )
+
+
 def add_parts(message, total):
     pair = message[:, PAIRS - 1].astype(F32) + three_parts(total)[0:2][None]
     message[:, PAIRS - 1] = pair.astype(BF16)
 
 
-def relay_kernel(recv, send_in, send_out):
+def places_early():
+    return lax.axis_index("level") < WAITING
+
+
+def relay_kernel(recv, own, send_in, send_out, base):
     del send_in
     add_parts(send_out, sum_parts(last_pair(recv, slice(None))[1:2])[0:1])
+
+    @pl.when(places_early())
+    def _():
+        base[...] = own[...] + placed(recv)
+
+    @pl.when(jnp.logical_not(places_early()))
+    def _():
+        base[...] = own[...]
 
 
 def placed(recv):
@@ -205,8 +228,13 @@
     return total
 
 
-def final_kernel(early, late, own, out, totals):
-    out[...] = own[...] + placed(early) + placed(late)
+def final_kernel(early, late, base, out, totals):
+    out[...] = base[...] + placed(late)
+
+    @pl.when(jnp.logical_not(places_early()))
+    def _():
+        out[...] += placed(early)
+
     both = sum_parts(last_pair(late, slice(None))[1:2])
     both = both + pltpu.roll(both, CELLS - COMP, 1)
     totals[...] = both[0:1, 0:COMP] * (1.0 / (CELLS * BLK))
@@ -242,7 +270,7 @@
     anywhere = pl.BlockSpec(memory_space=pl.ANY)
     vmem = pl.BlockSpec(memory_space=pltpu.VMEM)
     send_dev, send_lev, own = pl.pallas_call(
-        terms_kernel,
+        scoped_terms,
         name="terms",
         in_specs=[anywhere] * 11,
         out_specs=[vmem] * 3,
@@ -267,8 +295,6 @@
             pltpu.SMEM((CAP, levels), jnp.int32),
             pltpu.SMEM((CAP, levels), jnp.int32),
             pltpu.SMEM((1, levels), jnp.int32),
-            pltpu.SemaphoreType.DMA((8,)),
-            pltpu.SemaphoreType.DMA((W_CHUNKS + 2,)),
         ],
     )(
         flat,
@@ -286,14 +312,14 @@
     sends = {"dev": send_dev, "level": send_lev}
     early = exchange(sends[ORDER[0]], ORDER[0])
     second = sends[ORDER[1]]
-    second = pl.pallas_call(
+    second, base = pl.pallas_call(
         relay_kernel,
         name="relay",
-        in_specs=[vmem, vmem],
-        out_specs=vmem,
-        out_shape=pltpu.VMEM(second.shape, BF16),
-        input_output_aliases={1: 0},
-    )(early, in_vmem(second))
+        in_specs=[vmem] * 3,
+        out_specs=[vmem] * 2,
+        out_shape=[pltpu.VMEM(second.shape, BF16), pltpu.VMEM((rows, CELLS), F32)],
+        input_output_aliases={2: 0},
+    )(early, in_vmem(own), in_vmem(second))
     late = exchange(second, ORDER[1])
     remapped, totals = pl.pallas_call(
         final_kernel,
@@ -304,7 +330,7 @@
             jax.ShapeDtypeStruct((rows, CELLS), F32),
             jax.ShapeDtypeStruct((1, COMP), F32),
         ],
-    )(early, late, in_vmem(own))
+    )(early, late, in_vmem(base))
     remapped = jnp.transpose(remapped.reshape(COMP, BLK, CELLS), (1, 0, 2))
     return (remapped[None], totals.reshape(COMP))
 

time: 41 us -> 40.7 us (level)
  no operation moved by 1% of the time
where the time goes in v4:
time: 40.7 us; the launch traced here: 40.3 us
  blocking collectives  35.5 us (87%)
  Pallas kernels  4.12 us (10%)
  between operations  0.65 us (2%)
    all_to_all x2, blocking collectives, exchange(): lax.all_to_all(in_vmem(message), axis, 0, 0, axis_index_groups=groups, ti...  35.5 us
    pallas_call x1, Pallas kernels, body(): pl.pallas_call(scoped_terms, name='terms', in_specs=[anywhere] * 11, out_...  2.71 us
    pallas_call x1, Pallas kernels, body(): pl.pallas_call(final_kernel, name='final', in_specs=[vmem, vmem, vmem], o...  0.91 us

profile of v4, /device:TPU:1, one launch (start us, length us, event | category | flops | bytes accessed | tf_op | source)
XLA Modules:
  0.0 40.3 jit_solution(14851404129001265695)
XLA Ops:
  0.6 2.7 %terms.1 = (bf16[32,13,2,128]{3,2,1,0:T(2,128)(2,1)S(1)}, bf16[16,13,2,128]{3,2,1,0:T(2,128)(2,1)S(1)}, f32[192,128]{1,0:T(8,128)S(1)}) custom-call(f32[192,128]{1,0:T(8,128)} %bitcast.31, s32[1,16]{1,0:T(1,128)} %refs_1_.1, bf16[16,128,128]{2,1,0:T(8,128)(2,1)} %bitcast.30, s32[2,32]{1,0:T(2,128)} %bitcast.32, s32[2,32]{1,0:T(2,128)} %bitcast.33, ...), custom_call_target="tpu_custom_call" | custom-call | tf_op jit(solution)/shard_map/terms/pallas_call | solution.py:272
  3.4 16.9 %all_to_all.10.recv.early = bf16[32,13,2,128]{3,2,1,0:T(2,128)(2,1)S(1)} all-to-all(bf16[32,13,2,128]{3,2,1,0:T(2,128)(2,1)S(1)} %get-tuple-element.9), channel_id=1, replica_groups={{21,22,23,24,25,26,27,28,29,30,31,0,1,2,3,4,5,6,7,8,9,10,11,12,13,14,15..., dimensions={0} | all-to-all | bytes 425984 | tf_op jit(solution)/shard_map/all_to_all | solution.py:249
  20.2 0.5 %relay.1 = (bf16[16,13,2,128]{3,2,1,0:T(2,128)(2,1)S(1)}, f32[192,128]{1,0:T(8,128)S(1)}) custom-call(bf16[32,13,2,128]{3,2,1,0:T(2,128)(2,1)S(1)} %all_to_all.10.recv.early, f32[192,128]{1,0:T(8,128)S(1)} %get-tuple-element.10.own, bf16[16,13,2,128]{3,2,1,0:T(2,128)(2,1)S(1)} %get-tuple-element.11.send_in), custom_call_target="tpu_custom_call", output_to_operand_aliasing={{0}: (2, {})} | custom-call | tf_op jit(solution)/shard_map/relay/pallas_call | solution.py:315
  20.7 18.7 %all_to_all.11.late = bf16[16,13,2,128]{3,2,1,0:T(2,128)(2,1)S(1)} all-to-all(bf16[16,13,2,128]{3,2,1,0:T(2,128)(2,1)S(1)} %get-tuple-element.12), channel_id=1, replica_groups={{320,0,32,64,96,480,128,448,160,416,192,384,224,352,256,288},{321,1,33,..., dimensions={0} | all-to-all | bytes 212992 | tf_op jit(solution)/shard_map/all_to_all | solution.py:249
  39.4 0.9 %final.1 = (f32[192,128]{1,0:T(8,128)}, f32[1,12]{1,0:T(1,128)}) custom-call(bf16[32,13,2,128]{3,2,1,0:T(2,128)(2,1)S(1)} %all_to_all.10.recv.early, bf16[16,13,2,128]{3,2,1,0:T(2,128)(2,1)S(1)} %all_to_all.11.late, f32[192,128]{1,0:T(8,128)S(1)} %get-tuple-element.13.base), custom_call_target="tpu_custom_call" | custom-call | tf_op jit(solution)/shard_map/final/pallas_call | solution.py:324

commit v5 on v4

--- a/solution.py
+++ b/solution.py
@@ -173,15 +173,11 @@
         weights[n].wait()
         for peer in range(n * step, (n + 1) * step):
             acc = dev_step(peer, acc)
-    own_acc = jnp.concatenate([own_acc, jnp.zeros((8, CELLS), F32)], axis=0)
-    acc = jnp.concatenate([acc + own_acc, jnp.zeros((CELLS - 24, CELLS), F32)], axis=0)
-    sums = lax.dot_general(
-        jnp.ones((8, CELLS), F32),
-        acc,
-        (((1,), (1,)), ((), ())),
-        precision=lax.Precision.HIGHEST,
-        preferred_element_type=F32,
-    )
+    acc = acc + jnp.concatenate([own_acc, jnp.zeros((8, CELLS), F32)], axis=0)
+    row = lax.broadcasted_iota(jnp.int32, acc.shape, 0)
+    lane = lax.broadcasted_iota(jnp.int32, acc.shape, 1)
+    sums = jnp.where(row == lane, jnp.sum(acc, axis=1, keepdims=True), jnp.zeros_like(acc))
+    sums = jnp.sum(sums, axis=0, keepdims=True)
     add_parts(out_dev if ORDER[0] == "dev" else out_lev, sums[0:1])
 
 

time: 40.7 us -> 40.6 us (level)
  no operation moved by 1% of the time
where the time goes in v5:
time: 40.6 us; the launch traced here: 40.2 us
  blocking collectives  35.5 us (87%)
  Pallas kernels  4.05 us (10%)
  between operations  0.65 us (2%)
    all_to_all x2, blocking collectives, exchange(): lax.all_to_all(in_vmem(message), axis, 0, 0, axis_index_groups=groups, ti...  35.5 us
    pallas_call x1, Pallas kernels, body(): pl.pallas_call(scoped_terms, name='terms', in_specs=[anywhere] * 11, out_...  2.64 us
    pallas_call x1, Pallas kernels, body(): pl.pallas_call(final_kernel, name='final', in_specs=[vmem, vmem, vmem], o...  0.91 us

profile of v5, /device:TPU:1, one launch (start us, length us, event | category | flops | bytes accessed | tf_op | source)
XLA Modules:
  0.0 40.2 jit_solution(2344724664352252775)
XLA Ops:
  0.6 2.6 %terms.1 = (bf16[32,13,2,128]{3,2,1,0:T(2,128)(2,1)S(1)}, bf16[16,13,2,128]{3,2,1,0:T(2,128)(2,1)S(1)}, f32[192,128]{1,0:T(8,128)S(1)}) custom-call(f32[192,128]{1,0:T(8,128)} %bitcast.31, s32[1,16]{1,0:T(1,128)} %refs_1_.1, bf16[16,128,128]{2,1,0:T(8,128)(2,1)} %bitcast.30, s32[2,32]{1,0:T(2,128)} %bitcast.32, s32[2,32]{1,0:T(2,128)} %bitcast.33, ...), custom_call_target="tpu_custom_call" | custom-call | tf_op jit(solution)/shard_map/terms/pallas_call | solution.py:268
  3.3 16.9 %all_to_all.10.recv.early = bf16[32,13,2,128]{3,2,1,0:T(2,128)(2,1)S(1)} all-to-all(bf16[32,13,2,128]{3,2,1,0:T(2,128)(2,1)S(1)} %get-tuple-element.9), channel_id=1, replica_groups={{21,22,23,24,25,26,27,28,29,30,31,0,1,2,3,4,5,6,7,8,9,10,11,12,13,14,15..., dimensions={0} | all-to-all | bytes 425984 | tf_op jit(solution)/shard_map/all_to_all | solution.py:245
  20.2 0.5 %relay.1 = (bf16[16,13,2,128]{3,2,1,0:T(2,128)(2,1)S(1)}, f32[192,128]{1,0:T(8,128)S(1)}) custom-call(bf16[32,13,2,128]{3,2,1,0:T(2,128)(2,1)S(1)} %all_to_all.10.recv.early, f32[192,128]{1,0:T(8,128)S(1)} %get-tuple-element.10.own, bf16[16,13,2,128]{3,2,1,0:T(2,128)(2,1)S(1)} %get-tuple-element.11.send_in), custom_call_target="tpu_custom_call", output_to_operand_aliasing={{0}: (2, {})} | custom-call | tf_op jit(solution)/shard_map/relay/pallas_call | solution.py:311
  20.7 18.7 %all_to_all.11.late = bf16[16,13,2,128]{3,2,1,0:T(2,128)(2,1)S(1)} all-to-all(bf16[16,13,2,128]{3,2,1,0:T(2,128)(2,1)S(1)} %get-tuple-element.12), channel_id=1, replica_groups={{320,0,32,64,96,480,128,448,160,416,192,384,224,352,256,288},{321,1,33,..., dimensions={0} | all-to-all | bytes 212992 | tf_op jit(solution)/shard_map/all_to_all | solution.py:245
  39.3 0.9 %final.1 = (f32[192,128]{1,0:T(8,128)}, f32[1,12]{1,0:T(1,128)}) custom-call(bf16[32,13,2,128]{3,2,1,0:T(2,128)(2,1)S(1)} %all_to_all.10.recv.early, bf16[16,13,2,128]{3,2,1,0:T(2,128)(2,1)S(1)} %all_to_all.11.late, f32[192,128]{1,0:T(8,128)S(1)} %get-tuple-element.13.base), custom_call_target="tpu_custom_call" | custom-call | tf_op jit(solution)/shard_map/final/pallas_call | solution.py:320

commit v6 on v5

--- a/solution.py
+++ b/solution.py
@@ -190,8 +190,7 @@
 
 
 def add_parts(message, total):
-    pair = message[:, PAIRS - 1].astype(F32) + three_parts(total)[0:2][None]
-    message[:, PAIRS - 1] = pair.astype(BF16)
+    message[:, PAIRS - 1] += three_parts(total)[0:2].astype(BF16)[None]
 
 
 def places_early():

time: 40.6 us -> 40.6 us (level)
  no operation moved by 1% of the time
where the time goes in v6:
time: 40.6 us; the launch traced here: 40.2 us
  blocking collectives  35.6 us (88%)
  Pallas kernels  4.04 us (10%)
  between operations  0.65 us (2%)
    all_to_all x2, blocking collectives, exchange(): lax.all_to_all(in_vmem(message), axis, 0, 0, axis_index_groups=groups, ti...  35.6 us
    pallas_call x1, Pallas kernels, body(): pl.pallas_call(scoped_terms, name='terms', in_specs=[anywhere] * 11, out_...  2.63 us
    pallas_call x1, Pallas kernels, body(): pl.pallas_call(final_kernel, name='final', in_specs=[vmem, vmem, vmem], o...  0.91 us

profile of v6, /device:TPU:1, one launch (start us, length us, event | category | flops | bytes accessed | tf_op | source)
XLA Modules:
  0.0 40.2 jit_solution(12859564129878237479)
XLA Ops:
  0.6 2.6 %terms.1 = (bf16[32,13,2,128]{3,2,1,0:T(2,128)(2,1)S(1)}, bf16[16,13,2,128]{3,2,1,0:T(2,128)(2,1)S(1)}, f32[192,128]{1,0:T(8,128)S(1)}) custom-call(f32[192,128]{1,0:T(8,128)} %bitcast.31, s32[1,16]{1,0:T(1,128)} %refs_1_.1, bf16[16,128,128]{2,1,0:T(8,128)(2,1)} %bitcast.30, s32[2,32]{1,0:T(2,128)} %bitcast.32, s32[2,32]{1,0:T(2,128)} %bitcast.33, ...), custom_call_target="tpu_custom_call" | custom-call | tf_op jit(solution)/shard_map/terms/pallas_call | solution.py:267
  3.3 16.9 %all_to_all.10.recv.early = bf16[32,13,2,128]{3,2,1,0:T(2,128)(2,1)S(1)} all-to-all(bf16[32,13,2,128]{3,2,1,0:T(2,128)(2,1)S(1)} %get-tuple-element.9), channel_id=1, replica_groups={{21,22,23,24,25,26,27,28,29,30,31,0,1,2,3,4,5,6,7,8,9,10,11,12,13,14,15..., dimensions={0} | all-to-all | bytes 425984 | tf_op jit(solution)/shard_map/all_to_all | solution.py:244
  20.2 0.5 %relay.1 = (bf16[16,13,2,128]{3,2,1,0:T(2,128)(2,1)S(1)}, f32[192,128]{1,0:T(8,128)S(1)}) custom-call(bf16[32,13,2,128]{3,2,1,0:T(2,128)(2,1)S(1)} %all_to_all.10.recv.early, f32[192,128]{1,0:T(8,128)S(1)} %get-tuple-element.10.own, bf16[16,13,2,128]{3,2,1,0:T(2,128)(2,1)S(1)} %get-tuple-element.11.send_in), custom_call_target="tpu_custom_call", output_to_operand_aliasing={{0}: (2, {})} | custom-call | tf_op jit(solution)/shard_map/relay/pallas_call | solution.py:310
  20.7 18.7 %all_to_all.11.late = bf16[16,13,2,128]{3,2,1,0:T(2,128)(2,1)S(1)} all-to-all(bf16[16,13,2,128]{3,2,1,0:T(2,128)(2,1)S(1)} %get-tuple-element.12), channel_id=1, replica_groups={{320,0,32,64,96,480,128,448,160,416,192,384,224,352,256,288},{321,1,33,..., dimensions={0} | all-to-all | bytes 212992 | tf_op jit(solution)/shard_map/all_to_all | solution.py:244
  39.3 0.9 %final.1 = (f32[192,128]{1,0:T(8,128)}, f32[1,12]{1,0:T(1,128)}) custom-call(bf16[32,13,2,128]{3,2,1,0:T(2,128)(2,1)S(1)} %all_to_all.10.recv.early, bf16[16,13,2,128]{3,2,1,0:T(2,128)(2,1)S(1)} %all_to_all.11.late, f32[192,128]{1,0:T(8,128)S(1)} %get-tuple-element.13.base), custom_call_target="tpu_custom_call" | custom-call | tf_op jit(solution)/shard_map/final/pallas_call | solution.py:319
